TPU v7x, 32 devices: a whole 2x2x4 slice. The times are simulated.
32 devices in a mesh: blk: 16 (over z, y, core), grp: 2 (over x).
Axes of the slice: x: 2, y: 2, z: 4, core: 2. Of those that a mesh axis runs over, the one named last changes fastest.
Arguments:
- matrix_sat: float32 [512, 65536], P('grp', 'blk'), may hold values from -0.07883404 to 0.07883404
- matrix_ter: float32 [512, 65536], P('grp', 'blk'), may hold values from -0.07883404 to 0.07883404
- probes: float32 [16, 65536], P(None, 'blk'), may hold values from -6 to 6
Outputs:
- row_part: float32 [2, 16, 512], P(None, None, 'grp')
- column_part: float32 [2, 16, 65536], P(None, None, ('blk', 'grp'))
- trace_terms: float32 [2, 16], replicated
All inputs are finite; a program needn't handle non-finite values.
Results may differ from a plain program's by a relative error of at most 0.000096.
Values sent between devices are 32-bit elements; how exact they have to be, the bound alone decides.
A program may use at most 64 MiB of HBM per device.

v0:
```python
import jax
import jax.numpy as jnp
from jax import lax
from jax.sharding import PartitionSpec as P


def broadcast(block, axis, source):
    block = jnp.where(lax.axis_index(axis) == source, block, jnp.zeros_like(block))
    return lax.psum(block, axis)


def shards(matrix_sat, matrix_ter, probes):
    rows_dev, cols_dev = matrix_sat.shape
    column_index = lax.axis_index("blk")
    row_index = lax.axis_index("grp")
    row_ids = row_index * rows_dev + lax.broadcasted_iota(jnp.int32, (rows_dev, cols_dev), 0)
    col_ids = column_index * cols_dev + lax.broadcasted_iota(jnp.int32, (rows_dev, cols_dev), 1)
    upper_mask = col_ids >= row_ids
    strict_mask = col_ids > row_ids
    mine = lax.dynamic_slice_in_dim(probes, row_index * rows_dev, rows_dev, 1)
    slab_probes = broadcast(mine, "blk", 0)
    hp = lax.Precision.HIGHEST
    direct_list = []
    mirror_list = []
    for matrix in (matrix_sat, matrix_ter):
        masked_upper = jnp.where(upper_mask, matrix, 0.0)
        masked_strict = jnp.where(strict_mask, matrix, 0.0)
        direct_list.append(
            lax.dot_general(probes, masked_upper, (((1,), (1,)), ((), ())), precision=hp)
        )
        mirror_list.append(jnp.dot(slab_probes, masked_strict, precision=hp))
    direct_terms = jnp.stack(direct_list)
    mirror_terms = jnp.stack(mirror_list)
    early_local = jnp.sum(slab_probes[None] * direct_terms, axis=2) + jnp.sum(
        probes[None] * mirror_terms, axis=2
    )
    early_trace = lax.psum(early_local, ("blk", "grp"))
    row_part = lax.psum(direct_terms, "blk")
    column_part = lax.psum_scatter(mirror_terms, "grp", scatter_dimension=2, tiled=True)
    return (row_part, column_part, early_trace)


def solution(mesh):
    in_specs = (P("grp", "blk"), P("grp", "blk"), P(None, "blk"))
    out_specs = (P(None, None, "grp"), P(None, None, ("blk", "grp")), P())
    return jax.shard_map(shards, mesh=mesh, in_specs=in_specs, out_specs=out_specs, check_vma=False)
```

profile of v0, /device:TPU:0, one launch (start us, length us, event | category | flops | bytes accessed | tf_op | source)
XLA Modules:
  0.0 132.1 jit_solution(6201908092485074033)
XLA Ops:
  7.2 0.0 copy-start.2
  7.2 0.0 reduce-scatter.2.cloned.1.call-start
  7.2 0.0 copy-start
  7.3 5.8 %fusion.14 = f32[1,16,256]{2,1,0:T(8,128)S(1)} fusion(f32[16,4096]{1,0:T(8,128)} %param.5, f32[256,4096]{1,0:T(8,128)} %param.4, s32[4096]{0:T(1024)S(1)} %iota_add_fusion, s32[256]{0:T(256)S(1)} %iota_add_fusion.1), kind=kOutput, calls=%fused_computation.20 | convolution fusion | flops 203423744 | bytes 4490240 | tf_op jit(solution)/shard_map/dot_general | solution.py:29
  13.1 0.0 copy-done.2
  13.1 0.0 copy-done
  13.1 3.5 %fusion.15 = f32[1,16,256]{2,1,0:T(8,128)S(1)} fusion(f32[16,4096]{1,0:T(8,128)S(1)} %copy-done.2, f32[256,4096]{1,0:T(8,128)S(1)} %copy-done, s32[4096]{0:T(1024)S(1)} %iota_add_fusion, s32[256]{0:T(256)S(1)} %iota_add_fusion.1), kind=kOutput, calls=%fused_computation.21 | convolution fusion | flops 203423744 | bytes 4490240 | tf_op jit(solution)/shard_map/dot_general | solution.py:29
  16.6 63.7 %all-reduce = (f32[2,16,256]{2,1,0:T(8,128)}, f32[16,256]{1,0:T(8,128)S(1)}) all-reduce(f32[2,16,256]{2,1,0:T(8,128)S(1)} %pad_maximum_fusion.1, f32[16,256]{1,0:T(8,128)S(1)} %dynamic-slice_select_fusion), channel_id=1, replica_groups=mesh['blk'=16,'grp'=2] {'blk'}, use_global_device_ids=true, to_apply=%region_0.1 | all-reduce | flops 12288 | bytes 98304 | tf_op jit(solution)/shard_map/psum | solution.py:38
  80.3 0.0 copy-start.1
  80.3 4.7 %convolution_bitcast_fusion = f32[1,16,4096]{2,1,0:T(8,128)S(1)} fusion(f32[16,256]{1,0:T(8,128)S(1)} %get-tuple-element.4, f32[256,4096]{1,0:T(8,128)} %param.4, s32[4096]{0:T(1024)S(1)} %iota_add_fusion, s32[256]{0:T(256)S(1)} %iota_add_fusion.1), kind=kOutput, calls=%fused_computation.4 | convolution fusion | flops 203423744 | bytes 4490240 | tf_op jit(solution)/shard_map/dot_general | solution.py:31
  85.0 0.0 copy-done.1
  85.0 2.4 %convolution_bitcast_fusion.1 = f32[1,16,4096]{2,1,0:T(8,128)S(1)} fusion(f32[16,256]{1,0:T(8,128)S(1)} %get-tuple-element.4, f32[256,4096]{1,0:T(8,128)S(1)} %copy-done.1, s32[4096]{0:T(1024)S(1)} %iota_add_fusion, s32[256]{0:T(256)S(1)} %iota_add_fusion.1), kind=kOutput, calls=%fused_computation.5 | convolution fusion | flops 203423744 | bytes 4490240 | tf_op jit(solution)/shard_map/dot_general | solution.py:31
  87.4 0.9 multiply_reduce_fusion
  88.2 0.0 reduce-scatter.2.cloned.1.call-update
  88.2 0.1 multiply_reduce_fusion.1
  88.3 37.0 %psum.23 = f32[2,16]{1,0:T(2,128)} all-reduce(f32[2,16]{1,0:T(2,128)S(1)} %add.33), channel_id=1, replica_groups=mesh['blk'=16,'grp'=2] {'blk','grp'}, use_global_device_ids=true, to_apply=%region_5.6 | all-reduce | flops 32 | bytes 256 | tf_op jit(solution)/shard_map/psum | solution.py:37
  125.3 0.0 reduce-scatter.2.cloned.1.call-done
  (5 shorter events, 0.0 us)
Async XLA Ops:
  7.2 5.9 %copy-start.2 = (f32[16,4096]{1,0:T(8,128)S(1)}, f32[16,4096]{1,0:T(8,128)}, u32[]{:S(2)}) copy-start(f32[16,4096]{1,0:T(8,128)} %param.5) | copy-start | bytes 786436
  7.2 118.1 %reduce-scatter.2.cloned.1.call-start = ((), (), s32[]{:S(2)}) async-start(), calls=%async_computation.1 | async-start | bytes 786432 | tf_op jit(solution)/shard_map/reduce_scatter | solution.py:39
  7.2 5.9 %copy-start = (f32[256,4096]{1,0:T(8,128)S(1)}, f32[256,4096]{1,0:T(8,128)}, u32[]{:S(2)}) copy-start(f32[256,4096]{1,0:T(8,128)} %param.3) | copy-start | bytes 12582916
  80.3 4.7 %copy-start.1 = (f32[256,4096]{1,0:T(8,128)S(1)}, f32[256,4096]{1,0:T(8,128)}, u32[]{:S(2)}) copy-start(f32[256,4096]{1,0:T(8,128)} %param.3) | copy-start | bytes 12582916
Sparse Core Ops, SparseCore 0:
  88.4 12.2 reduce-scatter.1
where the time goes:
time: 133 us; the launch traced here: 132 us
  blocking collectives  101 us (76%)
  matrix products  16.3 us (12%)
  between operations  14.1 us (11%)
    psum x1, blocking collectives, shards(): row_part = lax.psum(direct_terms, 'blk')  63.7 us
    psum x1, blocking collectives, shards(): early_trace = lax.psum(early_local, ('blk', 'grp'))  37 us
    dot_general x2, matrix products, shards(): lax.dot_general(probes, masked_upper, (((1,), (1,)), ((), ())), precision...  9.25 us
    dot_general x2, matrix products, shards(): mirror_list.append(jnp.dot(slab_probes, masked_strict, precision=hp))  7.08 us
  transfers between devices with their start and end apart: 1, of which 0 were waited for; matrix products, arithmetic and copies ran while one was open for 0% of the time, Pallas kernels for 0%

commit v1 on v0

v1 whole, which is shorter than its diff:
```python
import functools

import jax
import jax.numpy as jnp
from jax import lax
from jax.experimental import pallas as pl
from jax.experimental.pallas import tpu as pltpu
from jax.sharding import PartitionSpec as P

MESH = pl.DeviceIdType.MESH
BF = jnp.bfloat16
F32 = jnp.float32


def halves(x):
    high = x.astype(BF)
    return high, (x - high.astype(F32)).astype(BF)


def kernel(nblk, ngrp, chunk, sub, sat_hbm, ter_hbm, probes_hbm, row_ref, col_ref, trace_ref,
           mats, high, low, probes, slab, tiles, parts, gathered, traces, outgoing, incoming,
           mat_sem, probe_sem, slab_sem, slab_send, slab_recv, one_send, one_recv, two_send, two_recv,
           trace_send, trace_recv, mirror_send, mirror_recv):
    blk, grp = lax.axis_index("blk"), lax.axis_index("grp")
    rows, cols = sat_hbm.shape
    nprobe = probes_hbm.shape[0]
    nchunk = cols // chunk
    width = cols // ngrp
    nsub = width // sub
    total = nblk * ngrp
    me = blk * ngrp + grp
    ntile = tiles.shape[0]
    lanes = rows // 128
    stride = nblk // ntile
    barrier = pltpu.get_barrier_semaphore()
    row0 = pl.multiple_of(grp * rows, rows)

    slab_copy = pltpu.make_async_copy(probes_hbm.at[:, pl.ds(row0, rows)], slab, slab_sem)
    pl.when(blk == 0)(slab_copy.start)
    probe_copy = pltpu.make_async_copy(probes_hbm, probes, probe_sem)
    probe_copy.start()
    loads = []
    for c in range(nchunk):
        for m, hbm in enumerate((sat_hbm, ter_hbm)):
            cut = pl.ds(c * chunk, chunk)
            load = pltpu.make_async_copy(hbm.at[:, cut], mats.at[m, :, cut], mat_sem.at[c, m])
            load.start()
            loads.append(load)

    def other(j):
        d = lax.rem(me + j, total)
        return (d // ngrp, lax.rem(d, ngrp))

    def greet(j, carry):
        pl.semaphore_signal(barrier, inc=1, device_id=other(j), device_id_type=MESH)
        return carry

    lax.fori_loop(1, total, greet, 0)

    def slab_to(j):
        return pltpu.make_async_remote_copy(
            src_ref=slab, dst_ref=slab, send_sem=slab_send.at[j], recv_sem=slab_recv,
            device_id=(jnp.int32(j), grp), device_id_type=MESH)

    @pl.when(blk == 0)
    def _():
        pl.semaphore_wait(barrier, total - 1)
        slab_copy.wait()
        for j in range(nblk - 1, 0, -1):
            slab_to(j).start()

    probe_copy.wait()
    p_high, p_low = halves(probes[...])
    p_both = jnp.concatenate([p_high, p_low], axis=0)
    contract = (((1,), (1,)), ((), ()))
    strict = [jnp.zeros((nprobe, rows), F32)] * 2
    waited = -(-(ngrp * rows) // chunk)
    for load in loads[:2 * waited]:
        load.wait()
    row_id = lax.broadcasted_iota(jnp.int32, (rows, rows), 0)
    col_id = lax.broadcasted_iota(jnp.int32, (rows, rows), 1)

    for m in range(2):
        @pl.when(blk == 0)
        def _():
            def clear(j, carry):
                mats[m, :, pl.ds(pl.multiple_of(j * rows, rows), rows)] = jnp.zeros((rows, rows), F32)
                return carry

            lax.fori_loop(0, grp, clear, 0)
            block = mats[m, :, pl.ds(row0, rows)]
            diagonal = jnp.sum(jnp.where(row_id == col_id, block, 0.0), axis=0, keepdims=True)
            row_ref[m] = slab[...] * diagonal
            mats[m, :, pl.ds(row0, rows)] = jnp.where(col_id > row_id, block, 0.0)

        @pl.when(blk != 0)
        def _():
            row_ref[m] = jnp.zeros((nprobe, rows), F32)

    for c in range(nchunk):
        cut = pl.ds(c * chunk, chunk)
        for m in range(2):
            if c >= waited:
                loads[2 * c + m].wait()
            m_high, m_low = halves(mats[m, :, cut])
            high[m, :, cut] = m_high
            low[m, :, cut] = m_low
            both = lax.dot_general(p_both[:, c * chunk:(c + 1) * chunk], m_high, contract, preferred_element_type=F32)
            rest = lax.dot_general(p_high[:, c * chunk:(c + 1) * chunk], m_low, contract, preferred_element_type=F32)
            strict[m] = strict[m] + ((both[nprobe:] + rest) + both[:nprobe])

    @pl.when(blk != 0)
    def _():
        pl.semaphore_wait(barrier, total - 1)

    upper = [strict[m] + row_ref[m] for m in range(2)]
    whole = jnp.concatenate(upper, axis=0)
    for k in range(ntile):
        i, j = k // lanes, k % lanes
        tiles[k] = whole[8 * i:8 * i + 8, 128 * j:128 * j + 128]

    def one_to(k):
        return pltpu.make_async_remote_copy(
            src_ref=tiles.at[k], dst_ref=parts.at[blk], send_sem=one_send.at[k], recv_sem=one_recv,
            device_id=(jnp.int32(k * stride), grp), device_id_type=MESH)

    for k in range(ntile):
        @pl.when(blk == k * stride)
        def _():
            parts[k * stride] = tiles[k]

        @pl.when(blk != k * stride)
        def _():
            one_to(k).start()

    @pl.when(blk != 0)
    def _():
        pltpu.make_async_remote_copy(
            src_ref=slab, dst_ref=slab, send_sem=slab_send.at[0], recv_sem=slab_recv,
            device_id=(jnp.int32(0), grp), device_id_type=MESH).wait_recv()

    s = slab[...]
    s_high, s_low = halves(s)
    s_both = jnp.concatenate([s_high, s_low], axis=0)

    def mirror(m, start):
        cut = pl.ds(pl.multiple_of(start, sub), sub)
        both = jnp.dot(s_both, high[m, :, cut], preferred_element_type=F32)
        rest = jnp.dot(s_high, low[m, :, cut], preferred_element_type=F32)
        return (both[nprobe:] + rest) + both[:nprobe]

    def mirror_to(k, q):
        return pltpu.make_async_remote_copy(
            src_ref=outgoing.at[k - 1, q], dst_ref=incoming.at[k - 1, q],
            send_sem=mirror_send.at[k - 1, q], recv_sem=mirror_recv.at[k - 1, q],
            device_id=(blk, lax.rem(grp + k, ngrp)), device_id_type=MESH)

    def trace_to(j):
        return pltpu.make_async_remote_copy(
            src_ref=traces.at[me], dst_ref=traces.at[me], send_sem=trace_send, recv_sem=trace_recv,
            device_id=other(j), device_id_type=MESH)

    def send_trace():
        share = jnp.concatenate([s * (upper[m] + strict[m]) for m in range(2)], axis=0)
        share = jnp.sum(share, axis=1, keepdims=True)
        n = 2 * nprobe
        spot = lax.broadcasted_iota(jnp.int32, (n, 128), 0) == lax.broadcasted_iota(jnp.int32, (n, 128), 1)
        traces[me] = jnp.sum(jnp.where(spot, share, 0.0), axis=0, keepdims=True)

        def go(j, carry):
            trace_to(j).start()
            return carry

        lax.fori_loop(1, total, go, 0)

    for k in range(1, ngrp):
        base = lax.rem(grp + k, ngrp) * width
        for q in range(nsub):
            for m in range(2):
                outgoing[k - 1, q, m] = mirror(m, base + q * sub)
            mirror_to(k, q).start()
            if k == 1 and q == 0:
                send_trace()

    for q in range(nsub):
        for m in range(2):
            col_ref[m, :, q * sub:(q + 1) * sub] = mirror(m, grp * width + q * sub)

    def two_to(k, j):
        return pltpu.make_async_remote_copy(
            src_ref=gathered.at[k], dst_ref=gathered.at[k], send_sem=two_send.at[j], recv_sem=two_recv.at[k],
            device_id=(lax.rem(blk + j, nblk), grp), device_id_type=MESH)

    for k in range(ntile):
        @pl.when(blk == k * stride)
        def _():
            few = parts.at[pl.ds(0, nblk - 1)]
            pltpu.make_async_copy(few, few, one_recv).wait()
            got = parts[0]
            for b in range(1, nblk):
                got = got + parts[b]
            gathered[k] = got
            for j in range(1, nblk):
                two_to(k, j).start()

    for k in range(1, ngrp):
        for q in range(nsub):
            mirror_to(k, q).wait_recv()
            for m in range(2):
                cut = slice(q * sub, (q + 1) * sub)
                col_ref[m, :, cut] = col_ref[m, :, cut] + incoming[k - 1, q, m]

    most = traces.at[pl.ds(0, total - 1)]
    pltpu.make_async_copy(most, most, trace_recv).wait()
    line = jnp.sum(traces[...], axis=0)
    for m in range(2):
        trace_ref[m:m + 1, :] = line[:, m * nprobe:(m + 1) * nprobe]

    for k in range(ntile):
        @pl.when(blk != k * stride)
        def _():
            two_to(k, 1).wait_recv()

        i, j = k // lanes, k % lanes
        m, r = (8 * i) // nprobe, (8 * i) % nprobe
        row_ref[m, r:r + 8, 128 * j:128 * j + 128] = gathered[k]

    @pl.when(blk == 0)
    def _():
        for j in range(nblk - 1, 0, -1):
            slab_to(j).wait_send()

    for k in range(ntile):
        @pl.when(blk != k * stride)
        def _():
            one_to(k).wait_send()

        @pl.when(blk == k * stride)
        def _():
            for j in range(1, nblk):
                two_to(k, j).wait_send()

    for k in range(1, ngrp):
        for q in range(nsub):
            mirror_to(k, q).wait_send()
    pltpu.make_async_copy(most, most, trace_send).wait()


def solution(mesh):
    nblk, ngrp = mesh.shape["blk"], mesh.shape["grp"]

    def shards(matrix_sat, matrix_ter, probes):
        rows, cols = matrix_sat.shape
        nprobe = probes.shape[0]
        chunk = min(1024, cols)
        width = cols // ngrp
        sub = min(512, width)
        nsub = width // sub
        ntile = (2 * nprobe // 8) * (rows // 128)
        far = max(ngrp - 1, 1)
        dma = pltpu.SemaphoreType.DMA
        hbm = pl.BlockSpec(memory_space=pltpu.MemorySpace.HBM)
        vmem = pl.BlockSpec(memory_space=pltpu.MemorySpace.VMEM)
        return tuple(pl.pallas_call(
            functools.partial(kernel, nblk, ngrp, chunk, sub),
            out_shape=[
                jax.ShapeDtypeStruct((2, nprobe, rows), F32),
                jax.ShapeDtypeStruct((2, nprobe, width), F32),
                jax.ShapeDtypeStruct((2, nprobe), F32),
            ],
            in_specs=[hbm] * 3,
            out_specs=[vmem] * 3,
            scratch_shapes=[
                pltpu.VMEM((2, rows, cols), F32),
                pltpu.VMEM((2, rows, cols), BF),
                pltpu.VMEM((2, rows, cols), BF),
                pltpu.VMEM((nprobe, cols), F32),
                pltpu.VMEM((nprobe, rows), F32),
                pltpu.VMEM((ntile, 8, 128), F32),
                pltpu.VMEM((nblk, 8, 128), F32),
                pltpu.VMEM((ntile, 8, 128), F32),
                pltpu.VMEM((nblk * ngrp, 1, 128), F32),
                pltpu.VMEM((far, nsub, 2, nprobe, sub), F32),
                pltpu.VMEM((far, nsub, 2, nprobe, sub), F32),
                dma((cols // chunk, 2)),
                dma, dma,
                dma((nblk,)), dma,
                dma((ntile,)), dma,
                dma((nblk,)), dma((ntile,)),
                dma, dma,
                dma((far, nsub)), dma((far, nsub)),
            ],
            compiler_params=pltpu.CompilerParams(
                collective_id=0, has_side_effects=True, vmem_limit_bytes=48 * 1024 * 1024),
            name="trace_step",
        )(matrix_sat, matrix_ter, probes))

    in_specs = (P("grp", "blk"), P("grp", "blk"), P(None, "blk"))
    out_specs = (P(None, None, "grp"), P(None, None, ("blk", "grp")), P())
    return jax.shard_map(shards, mesh=mesh, in_specs=in_specs, out_specs=out_specs, check_vma=False)
```

time: 133 us -> 26.6 us (0.20)
  blocking collectives: 101 us -> 0 us
  Pallas kernels: 0 us -> 20.8 us
  matrix products: 16.3 us -> 0 us
  between operations: 14.1 us -> 0.65 us
  local copies, waits for them, and re-layouts: 0.03 us -> 5.01 us
    psum x2 -> x0, blocking collectives: 101 us -> none  [the longest x1 63.7 us: shards(): row_part = lax.psum(direct_terms, 'blk')]
    pallas_call x0 -> x1, Pallas kernels: none -> 20.8 us  [shards(): pl.pallas_call(functools.partial(kernel, nblk, ngrp, chunk, sub), out_sha...]
    dot_general x4 -> x0, matrix products: 16.3 us -> none  [the longest x2 9.25 us: shards(): lax.dot_general(probes, masked_upper, (((1,), (1,)), ((), ())), precision...]
    unnamed x6 -> x7, local copies, waits for them, and re-layouts: 0.03 us -> 5.01 us
  transfers between devices with their start and end apart: 1 -> 0, of which waited for: 0 -> 0; matrix products, arithmetic and copies ran while one was open for 0% -> 0% of each run, Pallas kernels for 0% -> 0%
where the time goes in v1:
time: 26.6 us; the launch traced here: 26.4 us
  Pallas kernels  20.8 us (78%)
  local copies, waits for them, and re-layouts  5.01 us (19%)
  between operations  0.65 us (2%)
    pallas_call x1, Pallas kernels, shards(): pl.pallas_call(functools.partial(kernel, nblk, ngrp, chunk, sub), out_sha...  20.8 us
    unnamed x7, local copies, waits for them, and re-layouts  5.01 us

profile of v1, /device:TPU:0, one launch (start us, length us, event | category | flops | bytes accessed | tf_op | source)
XLA Modules:
  0.0 26.4 jit_solution(6165837937734925336)
XLA Ops:
  0.6 0.0 copy-start
  0.6 2.2 %copy-done = f32[256,4096]{1,0:T(8,128)S(1)} copy-done((f32[256,4096]{1,0:T(8,128)S(1)}, f32[256,4096]{1,0:T(8,128)}, u32[]{:S(2)}) %copy-start) | copy-done | bytes 4194328
  2.8 0.0 copy-start.1
  2.8 0.9 %copy-done.1 = f32[16,4096]{1,0:T(8,128)S(1)} copy-done((f32[16,4096]{1,0:T(8,128)S(1)}, f32[16,4096]{1,0:T(8,128)}, u32[]{:S(2)}) %copy-start.1) | copy-done | bytes 262168
  3.8 20.8 %trace_step.1 = (f32[2,16,256]{2,1,0:T(8,128)S(1)}, f32[2,16,2048]{2,1,0:T(8,128)S(1)}, f32[2,16]{1,0:T(2,128)S(1)}) custom-call(f32[256,4096]{1,0:T(8,128)S(1)} %copy-done, f32[256,4096]{1,0:T(8,128)} %ter_hbm.1, f32[16,4096]{1,0:T(8,128)S(1)} %copy-done.1), custom_call_target="tpu_custom_call" | custom-call | tf_op jit(solution)/shard_map/trace_step/pallas_call | solution.py:264
  24.6 0.6 %copy.9 = f32[2,16,256]{2,1,0:T(8,128)} copy(f32[2,16,256]{2,1,0:T(8,128)S(1)} %get-tuple-element.6) | data formatting | bytes 65536
  25.2 0.7 %copy.10 = f32[2,16,2048]{2,1,0:T(8,128)} copy(f32[2,16,2048]{2,1,0:T(8,128)S(1)} %get-tuple-element.7) | data formatting | bytes 524288
  25.9 0.6 %copy.11 = f32[2,16]{1,0:T(2,128)} copy(f32[2,16]{1,0:T(2,128)S(1)} %get-tuple-element.8) | data formatting | bytes 256
Async XLA Ops:
  0.6 2.2 %copy-start = (f32[256,4096]{1,0:T(8,128)S(1)}, f32[256,4096]{1,0:T(8,128)}, u32[]{:S(2)}) copy-start(f32[256,4096]{1,0:T(8,128)} %sat_hbm.1) | copy-start | bytes 12582916
  2.8 0.9 %copy-start.1 = (f32[16,4096]{1,0:T(8,128)S(1)}, f32[16,4096]{1,0:T(8,128)}, u32[]{:S(2)}) copy-start(f32[16,4096]{1,0:T(8,128)} %probes_hbm.1) | copy-start | bytes 786436

commit v2 on v1

--- a/solution.py
+++ b/solution.py
@@ -18,17 +18,15 @@
 
 
 def kernel(nblk, ngrp, chunk, sub, sat_hbm, ter_hbm, probes_hbm, row_ref, col_ref, trace_ref,
-           mats, high, low, probes, slab, tiles, parts, gathered, traces, outgoing, incoming,
+           mats, high, low, probes, slab, tiles, parts, gathered, traces, finals, outgoing, incoming,
            mat_sem, probe_sem, slab_sem, slab_send, slab_recv, one_send, one_recv, two_send, two_recv,
-           trace_send, trace_recv, mirror_send, mirror_recv):
+           trace_send, trace_recv, final_send, final_recv, mirror_send, mirror_recv):
     blk, grp = lax.axis_index("blk"), lax.axis_index("grp")
     rows, cols = sat_hbm.shape
     nprobe = probes_hbm.shape[0]
     nchunk = cols // chunk
     width = cols // ngrp
     nsub = width // sub
-    total = nblk * ngrp
-    me = blk * ngrp + grp
     ntile = tiles.shape[0]
     lanes = rows // 128
     stride = nblk // ntile
@@ -47,27 +45,24 @@
             load.start()
             loads.append(load)
 
-    def other(j):
-        d = lax.rem(me + j, total)
-        return (d // ngrp, lax.rem(d, ngrp))
-
-    def greet(j, carry):
-        pl.semaphore_signal(barrier, inc=1, device_id=other(j), device_id_type=MESH)
-        return carry
-
-    lax.fori_loop(1, total, greet, 0)
+    def member(j):
+        return (lax.rem(blk + j, nblk), grp)
+
+    def peer(k):
+        return (blk, lax.rem(grp + k, ngrp))
+
+    friends = nblk - 1 + ngrp - 1
+    for j in range(1, nblk):
+        pl.semaphore_signal(barrier, inc=1, device_id=member(j), device_id_type=MESH)
+    for k in range(1, ngrp):
+        pl.semaphore_signal(barrier, inc=1, device_id=peer(k), device_id_type=MESH)
 
     def slab_to(j):
         return pltpu.make_async_remote_copy(
             src_ref=slab, dst_ref=slab, send_sem=slab_send.at[j], recv_sem=slab_recv,
             device_id=(jnp.int32(j), grp), device_id_type=MESH)
 
-    @pl.when(blk == 0)
-    def _():
-        pl.semaphore_wait(barrier, total - 1)
-        slab_copy.wait()
-        for j in range(nblk - 1, 0, -1):
-            slab_to(j).start()
+    pl.when(blk == 0)(slab_copy.wait)
 
     probe_copy.wait()
     p_high, p_low = halves(probes[...])
@@ -108,10 +103,16 @@
             both = lax.dot_general(p_both[:, c * chunk:(c + 1) * chunk], m_high, contract, preferred_element_type=F32)
             rest = lax.dot_general(p_high[:, c * chunk:(c + 1) * chunk], m_low, contract, preferred_element_type=F32)
             strict[m] = strict[m] + ((both[nprobe:] + rest) + both[:nprobe])
+        if c == max(nchunk - 2, 0):
+            @pl.when(blk == 0)
+            def _():
+                pl.semaphore_wait(barrier, friends)
+                for j in range(nblk - 1, 0, -1):
+                    slab_to(j).start()
 
     @pl.when(blk != 0)
     def _():
-        pl.semaphore_wait(barrier, total - 1)
+        pl.semaphore_wait(barrier, friends)
 
     upper = [strict[m] + row_ref[m] for m in range(2)]
     whole = jnp.concatenate(upper, axis=0)
@@ -153,25 +154,26 @@
         return pltpu.make_async_remote_copy(
             src_ref=outgoing.at[k - 1, q], dst_ref=incoming.at[k - 1, q],
             send_sem=mirror_send.at[k - 1, q], recv_sem=mirror_recv.at[k - 1, q],
-            device_id=(blk, lax.rem(grp + k, ngrp)), device_id_type=MESH)
+            device_id=peer(k), device_id_type=MESH)
 
     def trace_to(j):
         return pltpu.make_async_remote_copy(
-            src_ref=traces.at[me], dst_ref=traces.at[me], send_sem=trace_send, recv_sem=trace_recv,
-            device_id=other(j), device_id_type=MESH)
+            src_ref=traces.at[blk], dst_ref=traces.at[blk], send_sem=trace_send.at[j], recv_sem=trace_recv,
+            device_id=member(j), device_id_type=MESH)
 
     def send_trace():
         share = jnp.concatenate([s * (upper[m] + strict[m]) for m in range(2)], axis=0)
         share = jnp.sum(share, axis=1, keepdims=True)
         n = 2 * nprobe
         spot = lax.broadcasted_iota(jnp.int32, (n, 128), 0) == lax.broadcasted_iota(jnp.int32, (n, 128), 1)
-        traces[me] = jnp.sum(jnp.where(spot, share, 0.0), axis=0, keepdims=True)
-
-        def go(j, carry):
+        traces[blk] = jnp.sum(jnp.where(spot, share, 0.0), axis=0, keepdims=True)
+        for j in range(1, nblk):
             trace_to(j).start()
-            return carry
-
-        lax.fori_loop(1, total, go, 0)
+
+    def final_to(k):
+        return pltpu.make_async_remote_copy(
+            src_ref=finals.at[grp], dst_ref=finals.at[grp], send_sem=final_send.at[k], recv_sem=final_recv.at[k],
+            device_id=peer(k), device_id_type=MESH)
 
     for k in range(1, ngrp):
         base = lax.rem(grp + k, ngrp) * width
@@ -189,7 +191,7 @@
     def two_to(k, j):
         return pltpu.make_async_remote_copy(
             src_ref=gathered.at[k], dst_ref=gathered.at[k], send_sem=two_send.at[j], recv_sem=two_recv.at[k],
-            device_id=(lax.rem(blk + j, nblk), grp), device_id_type=MESH)
+            device_id=member(j), device_id_type=MESH)
 
     for k in range(ntile):
         @pl.when(blk == k * stride)
@@ -203,6 +205,12 @@
             for j in range(1, nblk):
                 two_to(k, j).start()
 
+    most = traces.at[pl.ds(0, nblk - 1)]
+    pltpu.make_async_copy(most, most, trace_recv).wait()
+    finals[grp] = jnp.sum(traces[...], axis=0)
+    for k in range(1, ngrp):
+        final_to(k).start()
+
     for k in range(1, ngrp):
         for q in range(nsub):
             mirror_to(k, q).wait_recv()
@@ -210,9 +218,9 @@
                 cut = slice(q * sub, (q + 1) * sub)
                 col_ref[m, :, cut] = col_ref[m, :, cut] + incoming[k - 1, q, m]
 
-    most = traces.at[pl.ds(0, total - 1)]
-    pltpu.make_async_copy(most, most, trace_recv).wait()
-    line = jnp.sum(traces[...], axis=0)
+    for k in range(1, ngrp):
+        final_to(k).wait_recv()
+    line = jnp.sum(finals[...], axis=0)
     for m in range(2):
         trace_ref[m:m + 1, :] = line[:, m * nprobe:(m + 1) * nprobe]
 
@@ -243,7 +251,19 @@
     for k in range(1, ngrp):
         for q in range(nsub):
             mirror_to(k, q).wait_send()
-    pltpu.make_async_copy(most, most, trace_send).wait()
+    for j in range(1, nblk):
+        trace_to(j).wait_send()
+    for k in range(1, ngrp):
+        final_to(k).wait_send()
+
+
+def put_out(row_in, col_in, trace_in, row_out, col_out, trace_out, sem):
+    pairs = ((col_in, col_out), (row_in, row_out), (trace_in, trace_out))
+    copies = [pltpu.make_async_copy(a, b, sem.at[i]) for i, (a, b) in enumerate(pairs)]
+    for copy in copies:
+        copy.start()
+    for copy in copies:
+        copy.wait()
 
 
 def solution(mesh):
@@ -261,7 +281,7 @@
         dma = pltpu.SemaphoreType.DMA
         hbm = pl.BlockSpec(memory_space=pltpu.MemorySpace.HBM)
         vmem = pl.BlockSpec(memory_space=pltpu.MemorySpace.VMEM)
-        return tuple(pl.pallas_call(
+        parts = pl.pallas_call(
             functools.partial(kernel, nblk, ngrp, chunk, sub),
             out_shape=[
                 jax.ShapeDtypeStruct((2, nprobe, rows), F32),
@@ -279,7 +299,8 @@
                 pltpu.VMEM((ntile, 8, 128), F32),
                 pltpu.VMEM((nblk, 8, 128), F32),
                 pltpu.VMEM((ntile, 8, 128), F32),
-                pltpu.VMEM((nblk * ngrp, 1, 128), F32),
+                pltpu.VMEM((nblk, 1, 128), F32),
+                pltpu.VMEM((ngrp, 1, 128), F32),
                 pltpu.VMEM((far, nsub, 2, nprobe, sub), F32),
                 pltpu.VMEM((far, nsub, 2, nprobe, sub), F32),
                 dma((cols // chunk, 2)),
@@ -287,13 +308,22 @@
                 dma((nblk,)), dma,
                 dma((ntile,)), dma,
                 dma((nblk,)), dma((ntile,)),
-                dma, dma,
+                dma((nblk,)), dma,
+                dma((ngrp,)), dma((ngrp,)),
                 dma((far, nsub)), dma((far, nsub)),
             ],
             compiler_params=pltpu.CompilerParams(
-                collective_id=0, has_side_effects=True, vmem_limit_bytes=48 * 1024 * 1024),
+                collective_id=0, has_side_effects=True, vmem_limit_bytes=67043328),
             name="trace_step",
-        )(matrix_sat, matrix_ter, probes))
+        )(matrix_sat, matrix_ter, probes)
+        return tuple(pl.pallas_call(
+            put_out,
+            out_shape=[jax.ShapeDtypeStruct(part.shape, F32) for part in parts],
+            in_specs=[vmem] * 3,
+            out_specs=[hbm] * 3,
+            scratch_shapes=[dma((3,))],
+            name="put_out",
+        )(*parts))
 
     in_specs = (P("grp", "blk"), P("grp", "blk"), P(None, "blk"))
     out_specs = (P(None, None, "grp"), P(None, None, ("blk", "grp")), P())

time: 26.6 us -> 23.7 us (0.89)
  local copies, waits for them, and re-layouts: 5.01 us -> 0 us
  Pallas kernels: 20.8 us -> 22.9 us
    unnamed x7 -> x0, local copies, waits for them, and re-layouts: 5.01 us -> none
    pallas_call x0 -> x1, Pallas kernels: none -> 1.68 us  [shards(): pl.pallas_call(put_out, out_shape=[jax.ShapeDtypeStruct(part.shape, F32)...]
    pallas_call x1, Pallas kernels: 20.8 us -> 21.2 us  [shards(): pl.pallas_call(functools.partial(kernel, nblk, ngrp, chunk, sub), out_sha...]
where the time goes in v2:
time: 23.7 us; the launch traced here: 23.5 us
  Pallas kernels  22.9 us (97%)
  between operations  0.64 us (3%)
    pallas_call x1, Pallas kernels, shards(): pl.pallas_call(functools.partial(kernel, nblk, ngrp, chunk, sub), out_sha...  21.2 us
    pallas_call x1, Pallas kernels, shards(): pl.pallas_call(put_out, out_shape=[jax.ShapeDtypeStruct(part.shape, F32)...  1.68 us

profile of v2, /device:TPU:0, one launch (start us, length us, event | category | flops | bytes accessed | tf_op | source)
XLA Modules:
  0.0 23.5 jit_solution(246110138953342831)
XLA Ops:
  0.6 21.2 %trace_step.1 = (f32[2,16,256]{2,1,0:T(8,128)}, f32[2,16,2048]{2,1,0:T(8,128)}, f32[2,16]{1,0:T(2,128)}) custom-call(f32[256,4096]{1,0:T(8,128)} %sat_hbm.1, f32[256,4096]{1,0:T(8,128)} %ter_hbm.1, f32[16,4096]{1,0:T(8,128)} %probes_hbm.1), custom_call_target="tpu_custom_call" | custom-call | tf_op jit(solution)/shard_map/trace_step/pallas_call | solution.py:284
  21.9 1.7 %put_out.1 = (f32[2,16,256]{2,1,0:T(8,128)}, f32[2,16,2048]{2,1,0:T(8,128)}, f32[2,16]{1,0:T(2,128)}) custom-call(f32[2,16,256]{2,1,0:T(8,128)} %get-tuple-element.6.row_in, f32[2,16,2048]{2,1,0:T(8,128)} %get-tuple-element.7.col_in, f32[2,16]{1,0:T(2,128)} %get-tuple-element.8.trace_in), custom_call_target="tpu_custom_call" | custom-call | tf_op jit(solution)/shard_map/put_out/pallas_call | solution.py:319
